TPU v7x, 32 devices: a whole 2x2x4 slice. The times are simulated.
32 devices in a mesh: dom: 16 (over z, x, core), rep: 2 (over y).
Axes of the slice: x: 2, y: 2, z: 4, core: 2. Of those that a mesh axis runs over, the one named last changes fastest.
Arguments:
- features: bfloat16 [131072, 128], P('dom'), may hold values from -6 to 6
- partition_map: int32 [131072], replicated, may hold values from 0 to 131071, as said below
- seed_ids: int32 [2048], P(('dom', 'rep')), may hold values from 0 to 131071, as said below
- hop1_ids: int32 [2048, 15], P(('dom', 'rep')), may hold values from 0 to 131071, as said below
- hop2_ids: int32 [2048, 15, 10], P(('dom', 'rep')), may hold values from 0 to 131071, as said below
- labels: int32 [2048], P(('dom', 'rep')), may hold values from 0 to 171
- self_one: bfloat16 [128, 256], replicated, may hold values from -0.5 to 0.5
- neigh_one: bfloat16 [128, 256], replicated, may hold values from -0.5 to 0.5
- bias_one: float32 [256], replicated, may hold values from -3 to 3
- self_two: bfloat16 [256, 172], replicated, may hold values from -0.375 to 0.375
- neigh_two: bfloat16 [256, 172], replicated, may hold values from -0.375 to 0.375
- bias_two: float32 [172], replicated, may hold values from -2 to 112, as said below
Outputs:
- seed_loss: float32 [2048], P(('dom', 'rep'))
- grad_self_one: float32 [128, 256], replicated
- grad_neigh_one: float32 [128, 256], replicated
- grad_bias_one: float32 [256], replicated
- grad_self_two: float32 [256, 172], replicated
- grad_neigh_two: float32 [256, 172], replicated
- grad_bias_two: float32 [172], replicated
Inputs may be any that keep to these rules, and one draw needn't show every extreme that they name: A permutation of 0 to 131071: node v is stored at position p = partition_map[v], in partition p // 8192, row p % 8192. Rows below 256 of each partition hold hub nodes. `seed_ids`: node ids. `hop1_ids`: node ids. `hop2_ids`: take one device's 64 seeds (an aligned block of seeds) with all their hop-1 and hop-2 ids, 10624 ids with repeats counted, and map them through partition_map: at most 2428 positions fall in any one partition, and at most 332 fall in rows 256 and above of any one partition. Every device reaches both bounds. `bias_two`: class biases.
All inputs are finite; a program needn't handle non-finite values.
Results may differ from a plain program's by a relative error of at most 0.003.
Values may be sent and summed in bfloat16 or wider, within the bound.
A program may use at most 128 MiB of HBM per device.

v0:
```python
import jax
import jax.numpy as jnp
from jax import lax
from jax.sharding import PartitionSpec as P

HOT_DEV = 256


def activate(values):
    return jax.nn.gelu(values, approximate=True)


def sage_terms(
    seed_rows,
    hop_rows,
    far_rows,
    labels,
    self_one,
    neigh_one,
    bias_one,
    self_two,
    neigh_two,
    bias_two,
):
    seed_count = seed_rows.shape[0]
    fan_one = hop_rows.shape[0] // seed_count
    feat_width = seed_rows.shape[1]
    hidden = self_one.shape[1]
    seed_mean = jnp.mean(
        hop_rows.reshape(seed_count, fan_one, feat_width), axis=1, dtype=jnp.float32
    ).astype(jnp.bfloat16)
    far_mean = jnp.mean(far_rows, axis=1, dtype=jnp.float32).astype(jnp.bfloat16)
    pre_seed = (
        jnp.dot(seed_rows, self_one, preferred_element_type=jnp.float32)
        + jnp.dot(seed_mean, neigh_one, preferred_element_type=jnp.float32)
        + bias_one
    )
    pre_hop = (
        jnp.dot(hop_rows, self_one, preferred_element_type=jnp.float32)
        + jnp.dot(far_mean, neigh_one, preferred_element_type=jnp.float32)
        + bias_one
    )
    act_seed, back_seed = jax.vjp(activate, pre_seed)
    act_hop, back_hop = jax.vjp(activate, pre_hop)
    hid_seed = act_seed.astype(jnp.bfloat16)
    hid_hop = act_hop.astype(jnp.bfloat16)
    hop_mean = jnp.mean(
        hid_hop.reshape(seed_count, fan_one, hidden), axis=1, dtype=jnp.float32
    ).astype(jnp.bfloat16)
    logits = (
        jnp.dot(hid_seed, self_two, preferred_element_type=jnp.float32)
        + jnp.dot(hop_mean, neigh_two, preferred_element_type=jnp.float32)
        + bias_two
    )
    peak_value = jnp.max(logits, axis=1, keepdims=True)
    shifted = logits - peak_value
    log_total = jnp.log(jnp.sum(jnp.exp(shifted), axis=1, keepdims=True))
    log_probs = shifted - log_total
    class_iota = lax.broadcasted_iota(jnp.int32, logits.shape, 1)
    target = (labels[:, None] == class_iota).astype(jnp.float32)
    seed_loss = -jnp.sum(log_probs * target, axis=1)
    d_logits = ((jnp.exp(log_probs) - target) / seed_count).astype(jnp.bfloat16)
    grad_self_two = jnp.dot(hid_seed.T, d_logits, preferred_element_type=jnp.float32)
    grad_neigh_two = jnp.dot(hop_mean.T, d_logits, preferred_element_type=jnp.float32)
    grad_bias_two = jnp.sum(d_logits.astype(jnp.float32), axis=0)
    d_hid_seed = jnp.dot(d_logits, self_two.T, preferred_element_type=jnp.float32)
    d_hop_mean = jnp.dot(d_logits, neigh_two.T, preferred_element_type=jnp.float32)
    d_pre_seed = back_seed(d_hid_seed)[0].astype(jnp.bfloat16)
    spread = jnp.broadcast_to(
        (d_hop_mean / fan_one)[:, None, :], (seed_count, fan_one, hidden)
    ).reshape(seed_count * fan_one, hidden)
    d_pre_hop = back_hop(spread)[0].astype(jnp.bfloat16)
    grad_self_one = jnp.dot(seed_rows.T, d_pre_seed, preferred_element_type=jnp.float32) + jnp.dot(
        hop_rows.T, d_pre_hop, preferred_element_type=jnp.float32
    )
    grad_neigh_one = jnp.dot(seed_mean.T, d_pre_seed, preferred_element_type=jnp.float32) + jnp.dot(
        far_mean.T, d_pre_hop, preferred_element_type=jnp.float32
    )
    grad_bias_one = jnp.sum(d_pre_seed.astype(jnp.float32), axis=0) + jnp.sum(
        d_pre_hop.astype(jnp.float32), axis=0
    )
    return (
        seed_loss,
        (
            grad_self_one,
            grad_neigh_one,
            grad_bias_one,
            grad_self_two,
            grad_neigh_two,
            grad_bias_two,
        ),
    )


def bucket_slots(owners, chosen, part_count):
    columns = lax.broadcasted_iota(jnp.int32, (owners.shape[0], part_count), 1)
    member = ((owners[:, None] == columns) & chosen[:, None]).astype(jnp.int32)
    running = jnp.cumsum(member, axis=0)
    return jnp.sum(running * member, axis=1) - 1


def request_table(owners, slots, local_rows, part_count, capacity):
    target_slot = jnp.where(slots >= 0, slots, capacity)
    table = jnp.zeros((part_count, capacity), jnp.int32)
    return table.at[owners, target_slot].set(local_rows, mode="drop")


def shards(
    features,
    partition_map,
    seed_ids,
    hop1_ids,
    hop2_ids,
    labels,
    self_one,
    neigh_one,
    bias_one,
    self_two,
    neigh_two,
    bias_two,
):
    part_count = lax.axis_size("dom")
    seed_count = seed_ids.shape[0]
    fan_one = hop1_ids.shape[1]
    fan_two = hop2_ids.shape[2]
    node_rows = features.shape[0]
    feat_width = features.shape[1]
    tree_rows = 1 + fan_one + fan_one * fan_two
    seed_unit = seed_count // part_count
    cold_cap = tree_rows // 2 * seed_unit
    wanted = jnp.concatenate([seed_ids, hop1_ids.reshape(-1), hop2_ids.reshape(-1)])
    position = partition_map[wanted]
    owners = position // node_rows
    local_rows = position % node_rows
    is_cold = local_rows >= HOT_DEV
    slots = bucket_slots(owners, is_cold, part_count)
    request = request_table(owners, slots, local_rows, part_count, cold_cap)
    arrived = lax.all_to_all(request, "dom", split_axis=0, concat_axis=0, tiled=True)
    returned = lax.all_to_all(features[arrived], "dom", split_axis=0, concat_axis=0, tiled=True)
    hub_rows = lax.all_gather(features[:HOT_DEV], "dom", axis=0, tiled=True)
    from_far = returned[owners, jnp.maximum(slots, 0)]
    from_hub = hub_rows[owners * HOT_DEV + jnp.minimum(local_rows, HOT_DEV - 1)]
    fetched = jnp.where(is_cold[:, None], from_far, from_hub)
    seed_rows = fetched[:seed_count]
    hop_rows = fetched[seed_count : seed_count * (1 + fan_one)]
    far_rows = fetched[seed_count * (1 + fan_one) :].reshape(
        seed_count * fan_one, fan_two, feat_width
    )
    seed_loss, grads = sage_terms(
        seed_rows,
        hop_rows,
        far_rows,
        labels,
        self_one,
        neigh_one,
        bias_one,
        self_two,
        neigh_two,
        bias_two,
    )
    grad_self_one, grad_neigh_one, grad_bias_one, grad_self_two, grad_neigh_two, grad_bias_two = (
        grads
    )
    summed = lax.psum(
        (
            grad_self_one,
            grad_neigh_one,
            grad_bias_one,
            grad_self_two,
            grad_neigh_two,
            grad_bias_two,
        ),
        ("dom", "rep"),
    )
    return (seed_loss, summed[0], summed[1], summed[2], summed[3], summed[4], summed[5])


def solution(mesh):
    return jax.shard_map(
        shards,
        mesh=mesh,
        in_specs=(
            P("dom", None),
            P(),
            P(("dom", "rep")),
            P(("dom", "rep"), None),
            P(("dom", "rep"), None, None),
            P(("dom", "rep")),
            P(),
            P(),
            P(),
            P(),
            P(),
            P(),
        ),
        out_specs=(P(("dom", "rep")), P(), P(), P(), P(), P(), P()),
        check_vma=False,
    )
```

profile of v0, /device:TPU:0, one launch (start us, length us, event | category | flops | bytes accessed | tf_op | source)
XLA Modules:
  0.0 499.8 jit_solution(7547511234379188678)
XLA Ops:
  7.2 1.2 copy.25
  8.4 0.3 concatenate.36
  8.7 0.8 copy.24
  9.5 0.1 concatenate.35
  9.7 0.8 concatenate.37
  10.4 0.1 fusion.30
  10.6 54.9 %gather_fusion = s32[10624]{0:T(1024)S(1)} fusion(s32[131072]{0:T(1024)S(1)} %copy-done, s32[11264]{0:T(1024)S(1)} %pad_clamp_fusion.1), kind=kCustom, calls=%fused_computation | custom fusion | bytes 127488 | tf_op jit(solution)/shard_map/gather | solution.py:132
  65.6 0.9 fusion.11
  66.6 9.2 %reduce-window.6 = s32[16,83,128]{2,1,0:T(8,128)S(1)} reduce-window(s32[16,83,128]{2,1,0:T(8,128)} %fusion.11, s32[]{:T(128)} %constant.33.clone.1), window={size=1x1x128 pad=0_0x0_0x127_0}, to_apply=%region_0.1 | reduce-window | flops 21587968 | bytes 1359876 | tf_op jit(solution)/shard_map/reduce-window
  75.8 0.6 slice_reduce_fusion
  76.3 0.2 reduce-window.9
  76.6 0.3 broadcast_add_fusion
  76.8 0.3 fusion.13
  77.1 0.8 or_reduce_fusion
  77.9 0.2 multiply_reduce_fusion
  78.1 0.2 and_reduce_fusion
  78.3 50.0 %scatter_custom_fusion = s32[5312]{0:T(1024)S(1)} fusion(s32[10624]{0:T(1024)S(1)} %broadcast_select_fusion.1, s32[10624]{0:T(1024)S(1)} %get-tuple-element.22, s32[]{:T(128)} %constant.33.clone.1), kind=kCustom, calls=%fused_computation.111 | custom fusion | bytes 21252
  128.3 0.1 all_to_all.11
  128.4 13.8 %all_to_all.17 = s32[16,1,332]{2,1,0:T(1,128)S(1)} all-to-all(s32[16,1,332]{2,1,0:T(1,128)S(1)} %all_to_all.11), channel_id=1, replica_groups=mesh['dom'=16,'rep'=2] {'dom'}, dimensions={0} | all-to-all | bytes 42496 | tf_op jit(solution)/shard_map/all_to_all | solution.py:138
  142.3 0.1 reshape.365
  142.4 11.6 %gather_fusion.1 = bf16[5312,128]{1,0:T(8,128)(2,1)} fusion(bf16[8192,128]{1,0:T(8,128)(2,1)S(1)} %copy-done.1, s32[6144]{0:T(1024)S(1)} %pad_clamp_fusion.2), kind=kCustom, calls=%fused_computation.1 | custom fusion | bytes 2740992 | tf_op jit(solution)/shard_map/gather | solution.py:139
  154.0 2.3 reshape.364
  156.3 4.4 all-to-all-start.1
  160.8 0.6 slice.20
  161.5 0.2 all-reduce.4.cloned.1.call-start
  161.7 47.2 %all-gather.2.cloned.1.call-done = bf16[4096,128]{1,0:T(8,128)(2,1)} async-done(((bf16[256,128]{1,0:T(8,128)(2,1)}), bf16[4096,128]{1,0:T(8,128)(2,1)}) %all-gather.2.cloned.1.call-update) | async-done | bytes 1048592 | tf_op jit(solution)/shard_map/all_gather | solution.py:140
  208.9 21.8 %gather_fusion.3 = bf16[10624,128]{1,0:T(8,128)(2,1)} fusion(bf16[4096,128]{1,0:T(8,128)(2,1)} %all-gather.2.cloned.1.call-done, s32[11264]{0:T(1024)S(1)} %pad_clamp_fusion), kind=kCustom, calls=%fused_computation.3 | custom fusion | bytes 5481984 | tf_op jit(solution)/shard_map/gather | solution.py:142
  230.7 1.7 copy.26
  232.4 76.5 %gather_fusion.2 = bf16[10624,128]{1,0:T(8,128)(2,1)} fusion(bf16[16,332,128]{2,0,1:T(8,128)(2,1)S(1)} %copy.26, s32[10624]{0:T(1024)S(1)} %get-tuple-element.19), kind=kCustom, calls=%fused_computation.2 | custom fusion | bytes 5524480 | tf_op jit(solution)/shard_map/gather | solution.py:141
  309.0 7.6 %broadcast_select_fusion = bf16[10624,128]{1,0:T(8,128)(2,1)S(1)} fusion(bf16[10624,128]{1,0:T(8,128)(2,1)} %gather_fusion.2, bf16[10624,128]{1,0:T(8,128)(2,1)} %gather_fusion.3, pred[10624]{0:T(1024)(128)(4,1)S(1)} %get-tuple-element.21), kind=kLoop, calls=%fused_computation.5 | loop fusion | flops 1359872 | bytes 8169856 | tf_op jit(solution)/shard_map/jit(_where)/select_n | solution.py:143
  316.5 2.4 slice_convert_fusion
  318.9 0.8 slice_convert_fusion.1
  319.7 1.3 fusion.17
  321.0 0.8 fusion.39
  321.8 6.6 %reshape.353 = f32[960,10,128]{2,1,0:T(8,128)} reshape(f32[9600,128]{1,0:T(8,128)} %slice_convert_fusion) | data formatting | bytes 9830400 | tf_op jit(solution)/shard_map/convert_element_type | solution.py:32
  328.4 5.3 %reduce_sum.83 = f32[960,128]{1,0:T(8,128)} reduce(f32[960,10,128]{2,1,0:T(8,128)} %reshape.353, f32[]{:T(128)} %constant.78.clone.1), dimensions={1}, to_apply=%region_5.6 | reduce | flops 1105920 | bytes 5406724 | tf_op jit(solution)/shard_map/reduce_sum | solution.py:32
  333.7 3.2 fusion.15
  336.9 2.3 reshape.354
  339.2 1.4 reduce_sum.84
  340.7 1.9 reshape.352
  342.5 1.1 reduce_sum.82
  343.6 1.0 fusion.2
  344.6 1.1 fusion.52
  345.7 0.3 fusion.55
  346.0 0.2 exponential_reduce_fusion
  346.2 0.2 convert_reduce_fusion.1
  346.4 0.1 convolution_multiply_fusion
  346.5 1.1 convert_reduce_fusion.2
  347.6 0.9 fusion.41
  348.5 0.9 fusion.51
  349.4 0.2 fusion.44
  349.6 0.2 fusion.37
  349.8 1.1 broadcast_in_dim.13
  350.9 2.3 reshape.346
  353.2 2.3 convert_reduce_fusion
  355.4 0.9 convolution_add_fusion.1
  356.4 0.9 convolution_add_fusion.2
  357.3 0.5 neg.3
  357.8 38.8 %all-reduce = (f32[256]{0:T(256)}, f32[172]{0:T(256)}) all-reduce(f32[256]{0:T(256)S(1)} %add.216, f32[172]{0:T(256)S(1)} %get-tuple-element.13), channel_id=1, replica_groups=mesh['dom'=16,'rep'=2] {'dom','rep'}, use_global_device_ids=true, to_apply=%region_14.15 | all-reduce | flops 428 | bytes 3424 | tf_op jit(solution)/shard_map/psum | solution.py:164
  396.6 90.0 %all-reduce.4.cloned.1.call-done = (f32[128,256]{1,0:T(8,128)}, f32[128,256]{1,0:T(8,128)}, f32[256,172]{0,1:T(8,128)}, f32[256,172]{0,1:T(8,128)}) async-done(((f32[128,256]{1,0:T(8,128)}, f32[128,256]{1,0:T(8,128)}, f32[256,172]{0,1:T(8,128)}, f32[256,172]{0,1:T(8,128)}), (f32[128,256]{1,0:T(8,128)}, f32[128,256]{1,0:T(8,128)}, f32[256,172]{0,1:T(8,128)}, ...) | async-done | bytes 614416 | tf_op jit(solution)/shard_map/psum | solution.py:164
  486.6 1.6 copy.33
  488.2 1.6 copy.34
  489.8 1.6 copy.35
  491.4 1.6 copy.36
  (38 shorter events, 0.4 us)
Async XLA Ops:
  7.2 3.4 copy-start
  65.6 12.3 %copy-start.10 = (s32[2]{0:T(128)S(1)}, s32[2]{0:T(128)}, u32[]{:S(2)}) copy-start(s32[2]{0:T(128)} %constant.89) | copy-start | bytes 28
  65.6 12.5 %copy-start.9 = (s32[2]{0:T(128)S(1)}, s32[2]{0:T(128)}, u32[]{:S(2)}) copy-start(s32[2]{0:T(128)} %constant.92) | copy-start | bytes 28
  66.6 75.8 %copy-start.1 = (bf16[8192,128]{1,0:T(8,128)(2,1)S(1)}, bf16[8192,128]{1,0:T(8,128)(2,1)}, u32[]{:S(2)}) copy-start(bf16[8192,128]{1,0:T(8,128)(2,1)} %param.12) | copy-start | bytes 6291460
  156.3 74.4 %all-to-all-start.1 = ((bf16[16,332,128]{2,1,0:T(8,128)(2,1)}), bf16[16,332,128]{2,1,0:T(8,128)(2,1)}, u32[]{:S(2)}, u32[]{:S(2)}) async-start(bf16[16,332,128]{2,1,0:T(8,128)(2,1)} %reshape.364), calls=%async_computation.1 | async-start | bytes 2752512 | tf_op jit(solution)/shard_map/all_to_all | solution.py:139
  160.7 48.2 %all-gather.2.cloned.1.call-start = ((), (), s32[]{:S(2)}) async-start(), calls=%async_computation.2 | async-start | bytes 1114112 | tf_op jit(solution)/shard_map/all_gather | solution.py:140
  161.5 325.2 %all-reduce.4.cloned.1.call-start = ((), (), s32[]{:S(2)}) async-start(), calls=%async_computation.3 | async-start | bytes 1245184 | tf_op jit(solution)/shard_map/psum | solution.py:164
  316.5 3.2 copy-start.5
  328.4 5.3 %copy-start.4 = (bf16[128,256]{1,0:T(8,128)(2,1)S(1)}, bf16[128,256]{1,0:T(8,128)(2,1)}, u32[]{:S(2)}) copy-start(bf16[128,256]{1,0:T(8,128)(2,1)} %param.19) | copy-start | bytes 196612
  328.4 5.3 %copy-start.6 = (f32[256]{0:T(256)S(1)}, f32[256]{0:T(256)}, u32[]{:S(2)}) copy-start(f32[256]{0:T(256)} %param.20) | copy-start | bytes 3076
  336.9 8.8 %copy-start.3 = (bf16[256,172]{0,1:T(8,128)(2,1)S(1)}, bf16[256,172]{0,1:T(8,128)(2,1)}, u32[]{:S(2)}) copy-start(bf16[256,172]{0,1:T(8,128)(2,1)} %param.22) | copy-start | bytes 264196
  336.9 8.8 %copy-start.7 = (f32[172]{0:T(256)S(1)}, f32[172]{0:T(256)}, u32[]{:S(2)}) copy-start(f32[172]{0:T(256)} %param.23) | copy-start | bytes 2068
  336.9 9.3 %copy-start.8 = (s32[64]{0:T(128)S(1)}, s32[64]{0:T(128)}, u32[]{:S(2)}) copy-start(s32[64]{0:T(128)} %param.17) | copy-start | bytes 772
  353.2 2.3 copy-start.2
Sparse Core Ops, SparseCore 0:
  164.3 44.5 all-gather.1
  357.4 129.1 all-reduce.3
where the time goes:
time: 502 us; the launch traced here: 500 us
  local copies, waits for them, and re-layouts  244 us (49%)
  waiting for transfers between devices  137 us (27%)
  blocking collectives  52.5 us (10%)
  other arithmetic  34.2 us (7%)
  between operations  14.3 us (3%)
  matrix products  12.8 us (3%)
    psum x1, waiting for transfers between devices, shards(): lax.psum((grad_self_one, grad_neigh_one, grad_bias_one, grad_self_two, gr...  90 us
    gather x1, local copies, waits for them, and re-layouts, shards(): from_far = returned[owners, jnp.maximum(slots, 0)]  76.5 us
    unnamed x29, local copies, waits for them, and re-layouts  58.4 us
    gather x1, local copies, waits for them, and re-layouts, shards(): position = partition_map[wanted]  54.9 us
    all_gather x1, waiting for transfers between devices, shards(): hub_rows = lax.all_gather(features[:HOT_DEV], 'dom', axis=0, tiled=True)  47.2 us
    psum x1, blocking collectives, shards(): lax.psum((grad_self_one, grad_neigh_one, grad_bias_one, grad_self_two, gr...  38.8 us
    gather x1, local copies, waits for them, and re-layouts, shards(): from_hub = hub_rows[owners * HOT_DEV + jnp.minimum(local_rows, HOT_DEV - 1)]  21.8 us
    gather x2, local copies, waits for them, and re-layouts, shards(): features[arrived]  13.9 us
  transfers between devices with their start and end apart: 3, of which 2 were waited for; matrix products, arithmetic and copies ran while one was open for 5% of the time, Pallas kernels for 0%

commit v1 on v0

--- a/solution.py
+++ b/solution.py
@@ -161,17 +161,16 @@
     grad_self_one, grad_neigh_one, grad_bias_one, grad_self_two, grad_neigh_two, grad_bias_two = (
         grads
     )
-    summed = lax.psum(
-        (
-            grad_self_one,
-            grad_neigh_one,
-            grad_bias_one,
-            grad_self_two,
-            grad_neigh_two,
-            grad_bias_two,
-        ),
-        ("dom", "rep"),
+    summed = (
+        grad_self_one,
+        grad_neigh_one,
+        grad_bias_one,
+        grad_self_two,
+        grad_neigh_two,
+        grad_bias_two,
     )
+    for ix in ("dom", "rep"):
+        summed = lax.psum(summed, axis_name=ix)
     return (seed_loss, summed[0], summed[1], summed[2], summed[3], summed[4], summed[5])
 
 

time: 502 us -> 501 us (level)
    psum x1 -> x2, blocking collectives: 38.8 us -> 37.1 us  [shards(): summed = lax.psum(summed, axis_name=ix)]
    psum x1 -> x2, waiting for transfers between devices: 90 us -> 91 us  [shards(): summed = lax.psum(summed, axis_name=ix)]
  transfers between devices with their start and end apart: 3 -> 4, of which waited for: 2 -> 2; matrix products, arithmetic and copies ran while one was open for 5% -> 5% of each run, Pallas kernels for 0% -> 0%
where the time goes in v1:
time: 501 us; the launch traced here: 499 us
  local copies, waits for them, and re-layouts  244 us (49%)
  waiting for transfers between devices  138 us (28%)
  blocking collectives  50.9 us (10%)
  other arithmetic  34.2 us (7%)
  between operations  14 us (3%)
  matrix products  12.8 us (3%)
    psum x2, waiting for transfers between devices, shards(): summed = lax.psum(summed, axis_name=ix)  91 us
    gather x1, local copies, waits for them, and re-layouts, shards(): from_far = returned[owners, jnp.maximum(slots, 0)]  76.5 us
    unnamed x29, local copies, waits for them, and re-layouts  58.4 us
    gather x1, local copies, waits for them, and re-layouts, shards(): position = partition_map[wanted]  54.9 us
    all_gather x1, waiting for transfers between devices, shards(): hub_rows = lax.all_gather(features[:HOT_DEV], 'dom', axis=0, tiled=True)  47.2 us
    psum x2, blocking collectives, shards(): summed = lax.psum(summed, axis_name=ix)  37.1 us
    gather x1, local copies, waits for them, and re-layouts, shards(): from_hub = hub_rows[owners * HOT_DEV + jnp.minimum(local_rows, HOT_DEV - 1)]  21.8 us
    gather x2, local copies, waits for them, and re-layouts, shards(): features[arrived]  13.9 us
  transfers between devices with their start and end apart: 4, of which 2 were waited for; matrix products, arithmetic and copies ran while one was open for 5% of the time, Pallas kernels for 0%

profile of v1, /device:TPU:0, one launch (start us, length us, event | category | flops | bytes accessed | tf_op | source)
XLA Modules:
  0.0 498.9 jit_solution(10463376944205172009)
XLA Ops:
  7.2 1.2 copy.25
  8.4 0.3 concatenate.36
  8.7 0.8 copy.24
  9.5 0.1 concatenate.35
  9.7 0.8 concatenate.37
  10.4 0.1 fusion.30
  10.6 54.9 %gather_fusion = s32[10624]{0:T(1024)S(1)} fusion(s32[131072]{0:T(1024)S(1)} %copy-done, s32[11264]{0:T(1024)S(1)} %pad_clamp_fusion.1), kind=kCustom, calls=%fused_computation | custom fusion | bytes 127488 | tf_op jit(solution)/shard_map/gather | solution.py:132
  65.6 0.9 fusion.11
  66.6 9.2 %reduce-window.6 = s32[16,83,128]{2,1,0:T(8,128)S(1)} reduce-window(s32[16,83,128]{2,1,0:T(8,128)} %fusion.11, s32[]{:T(128)} %constant.33.clone.1), window={size=1x1x128 pad=0_0x0_0x127_0}, to_apply=%region_0.1 | reduce-window | flops 21587968 | bytes 1359876 | tf_op jit(solution)/shard_map/reduce-window
  75.8 0.6 slice_reduce_fusion
  76.3 0.2 reduce-window.9
  76.6 0.3 broadcast_add_fusion
  76.8 0.3 fusion.13
  77.1 0.8 or_reduce_fusion
  77.9 0.2 multiply_reduce_fusion
  78.1 0.2 and_reduce_fusion
  78.3 50.0 %scatter_custom_fusion = s32[5312]{0:T(1024)S(1)} fusion(s32[10624]{0:T(1024)S(1)} %broadcast_select_fusion.1, s32[10624]{0:T(1024)S(1)} %get-tuple-element.28, s32[]{:T(128)} %constant.33.clone.1), kind=kCustom, calls=%fused_computation.111 | custom fusion | bytes 21252
  128.3 0.1 all_to_all.11
  128.4 13.8 %all_to_all.17 = s32[16,1,332]{2,1,0:T(1,128)S(1)} all-to-all(s32[16,1,332]{2,1,0:T(1,128)S(1)} %all_to_all.11), channel_id=1, replica_groups=mesh['dom'=16,'rep'=2] {'dom'}, dimensions={0} | all-to-all | bytes 42496 | tf_op jit(solution)/shard_map/all_to_all | solution.py:138
  142.4 11.6 %gather_fusion.1 = bf16[5312,128]{1,0:T(8,128)(2,1)} fusion(bf16[8192,128]{1,0:T(8,128)(2,1)S(1)} %copy-done.1, s32[6144]{0:T(1024)S(1)} %pad_clamp_fusion.2), kind=kCustom, calls=%fused_computation.1 | custom fusion | bytes 2740992 | tf_op jit(solution)/shard_map/gather | solution.py:139
  154.0 2.3 reshape.364
  156.3 4.4 all-to-all-start.1
  160.8 0.6 slice.20
  161.5 0.2 all-reduce.7.cloned.1.call-start
  161.7 47.2 %all-gather.2.cloned.1.call-done = bf16[4096,128]{1,0:T(8,128)(2,1)} async-done(((bf16[256,128]{1,0:T(8,128)(2,1)}), bf16[4096,128]{1,0:T(8,128)(2,1)}) %all-gather.2.cloned.1.call-update) | async-done | bytes 1048592 | tf_op jit(solution)/shard_map/all_gather | solution.py:140
  208.9 21.8 %gather_fusion.3 = bf16[10624,128]{1,0:T(8,128)(2,1)} fusion(bf16[4096,128]{1,0:T(8,128)(2,1)} %all-gather.2.cloned.1.call-done, s32[11264]{0:T(1024)S(1)} %pad_clamp_fusion), kind=kCustom, calls=%fused_computation.3 | custom fusion | bytes 5481984 | tf_op jit(solution)/shard_map/gather | solution.py:142
  230.7 1.7 copy.26
  232.4 76.5 %gather_fusion.2 = bf16[10624,128]{1,0:T(8,128)(2,1)} fusion(bf16[16,332,128]{2,0,1:T(8,128)(2,1)S(1)} %copy.26, s32[10624]{0:T(1024)S(1)} %get-tuple-element.25), kind=kCustom, calls=%fused_computation.2 | custom fusion | bytes 5524480 | tf_op jit(solution)/shard_map/gather | solution.py:141
  309.0 7.6 %broadcast_select_fusion = bf16[10624,128]{1,0:T(8,128)(2,1)S(1)} fusion(bf16[10624,128]{1,0:T(8,128)(2,1)} %gather_fusion.2, bf16[10624,128]{1,0:T(8,128)(2,1)} %gather_fusion.3, pred[10624]{0:T(1024)(128)(4,1)S(1)} %get-tuple-element.27), kind=kLoop, calls=%fused_computation.5 | loop fusion | flops 1359872 | bytes 8169856 | tf_op jit(solution)/shard_map/jit(_where)/select_n | solution.py:143
  316.5 2.4 slice_convert_fusion
  318.9 0.8 slice_convert_fusion.1
  319.7 1.3 fusion.17
  321.0 0.8 fusion.39
  321.8 6.6 %reshape.353 = f32[960,10,128]{2,1,0:T(8,128)} reshape(f32[9600,128]{1,0:T(8,128)} %slice_convert_fusion) | data formatting | bytes 9830400 | tf_op jit(solution)/shard_map/convert_element_type | solution.py:32
  328.4 5.3 %reduce_sum.83 = f32[960,128]{1,0:T(8,128)} reduce(f32[960,10,128]{2,1,0:T(8,128)} %reshape.353, f32[]{:T(128)} %constant.78.clone.1), dimensions={1}, to_apply=%region_5.6 | reduce | flops 1105920 | bytes 5406724 | tf_op jit(solution)/shard_map/reduce_sum | solution.py:32
  333.7 3.2 fusion.15
  336.9 2.3 reshape.354
  339.2 1.4 reduce_sum.84
  340.7 1.9 reshape.352
  342.5 1.1 reduce_sum.82
  343.6 1.0 fusion.2
  344.6 1.1 fusion.52
  345.7 0.3 fusion.55
  346.0 0.2 exponential_reduce_fusion
  346.2 0.2 convert_reduce_fusion.1
  346.4 0.1 convolution_multiply_fusion
  346.5 1.1 convert_reduce_fusion.2
  347.6 0.9 fusion.41
  348.5 0.9 fusion.51
  349.4 0.2 fusion.44
  349.6 0.2 fusion.37
  349.8 1.1 broadcast_in_dim.13
  350.9 2.3 reshape.346
  353.2 2.3 convert_reduce_fusion
  355.4 0.9 convolution_add_fusion.1
  356.4 0.9 convolution_add_fusion.2
  357.4 91.0 %all-reduce.7.cloned.1.call-done = (f32[128,256]{1,0:T(8,128)}, f32[128,256]{1,0:T(8,128)}, f32[256,172]{0,1:T(8,128)}, f32[256,172]{0,1:T(8,128)}) async-done(((f32[128,256]{1,0:T(8,128)}, f32[128,256]{1,0:T(8,128)}, f32[256,172]{0,1:T(8,128)}, f32[256,172]{0,1:T(8,128)}), (f32[128,256]{1,0:T(8,128)}, f32[128,256]{1,0:T(8,128)}, f32[256,172]{0,1:T(8,128)}, ...) | async-done | bytes 614416 | tf_op jit(solution)/shard_map/psum | solution.py:173
  448.4 0.5 neg.3
  448.9 31.6 %all-reduce = (f32[256]{0:T(256)S(1)}, f32[172]{0:T(256)S(1)}) all-reduce(f32[256]{0:T(256)S(1)} %add.228, f32[172]{0:T(256)S(1)} %get-tuple-element.19), channel_id=1, replica_groups=mesh['dom'=16,'rep'=2] {'dom'}, use_global_device_ids=true, to_apply=%region_16.17 | all-reduce | flops 428 | bytes 3424 | tf_op jit(solution)/shard_map/psum | solution.py:173
  480.5 5.5 %all-reduce.2 = (f32[256]{0:T(256)}, f32[172]{0:T(256)}) all-reduce(f32[256]{0:T(256)S(1)} %get-tuple-element.7, f32[172]{0:T(256)S(1)} %get-tuple-element.8), channel_id=1, replica_groups=mesh['dom'=16,'rep'=2] {'rep'}, use_global_device_ids=true, to_apply=%region_17.18 | all-reduce | flops 428 | bytes 3424 | tf_op jit(solution)/shard_map/psum | solution.py:173
  486.0 1.6 copy.37
  487.6 1.6 copy.38
  489.1 1.6 copy.39
  490.7 1.6 copy.40
  (42 shorter events, 0.6 us)
Async XLA Ops:
  7.2 3.4 copy-start
  65.6 12.3 %copy-start.10 = (s32[2]{0:T(128)S(1)}, s32[2]{0:T(128)}, u32[]{:S(2)}) copy-start(s32[2]{0:T(128)} %constant.89) | copy-start | bytes 28
  65.6 12.5 %copy-start.9 = (s32[2]{0:T(128)S(1)}, s32[2]{0:T(128)}, u32[]{:S(2)}) copy-start(s32[2]{0:T(128)} %constant.92) | copy-start | bytes 28
  66.6 75.8 %copy-start.1 = (bf16[8192,128]{1,0:T(8,128)(2,1)S(1)}, bf16[8192,128]{1,0:T(8,128)(2,1)}, u32[]{:S(2)}) copy-start(bf16[8192,128]{1,0:T(8,128)(2,1)} %param.12) | copy-start | bytes 6291460
  156.3 74.4 %all-to-all-start.1 = ((bf16[16,332,128]{2,1,0:T(8,128)(2,1)}), bf16[16,332,128]{2,1,0:T(8,128)(2,1)}, u32[]{:S(2)}, u32[]{:S(2)}) async-start(bf16[16,332,128]{2,1,0:T(8,128)(2,1)} %reshape.364), calls=%async_computation.1 | async-start | bytes 2752512 | tf_op jit(solution)/shard_map/all_to_all | solution.py:139
  160.7 48.2 %all-gather.2.cloned.1.call-start = ((), (), s32[]{:S(2)}) async-start(), calls=%async_computation.2 | async-start | bytes 1114112 | tf_op jit(solution)/shard_map/all_gather | solution.py:140
  161.5 286.9 %all-reduce.7.cloned.1.call-start = ((), (), s32[]{:S(2)}) async-start(), calls=%async_computation.3 | async-start | bytes 1245184 | tf_op jit(solution)/shard_map/psum | solution.py:173
  316.5 3.2 copy-start.5
  328.4 5.3 %copy-start.4 = (bf16[128,256]{1,0:T(8,128)(2,1)S(1)}, bf16[128,256]{1,0:T(8,128)(2,1)}, u32[]{:S(2)}) copy-start(bf16[128,256]{1,0:T(8,128)(2,1)} %param.19) | copy-start | bytes 196612
  328.4 5.3 %copy-start.6 = (f32[256]{0:T(256)S(1)}, f32[256]{0:T(256)}, u32[]{:S(2)}) copy-start(f32[256]{0:T(256)} %param.20) | copy-start | bytes 3076
  336.9 8.8 %copy-start.3 = (bf16[256,172]{0,1:T(8,128)(2,1)S(1)}, bf16[256,172]{0,1:T(8,128)(2,1)}, u32[]{:S(2)}) copy-start(bf16[256,172]{0,1:T(8,128)(2,1)} %param.22) | copy-start | bytes 264196
  336.9 8.8 %copy-start.7 = (f32[172]{0:T(256)S(1)}, f32[172]{0:T(256)}, u32[]{:S(2)}) copy-start(f32[172]{0:T(256)} %param.23) | copy-start | bytes 2068
  336.9 9.3 %copy-start.8 = (s32[64]{0:T(128)S(1)}, s32[64]{0:T(128)}, u32[]{:S(2)}) copy-start(s32[64]{0:T(128)} %param.17) | copy-start | bytes 772
  353.2 2.3 copy-start.2
  357.3 128.7 %all-reduce.9.cloned.1.call-start = ((), (), s32[]{:S(2)}) async-start(), calls=%async_computation.4 | async-start | bytes 1245184 | tf_op jit(solution)/shard_map/psum | solution.py:173
Sparse Core Ops, SparseCore 0:
  164.3 44.5 all-gather.1
  357.4 90.8 all-reduce.6
  450.8 31.0 all-reduce.8
